TPU v7x, 128 devices: a whole 4x4x4 slice. The times are simulated.
128 devices in a mesh: task: 2 (over core), row: 64 (over x, y, z).
Axes of the slice: x: 4, y: 4, z: 4, core: 2. Of those that a mesh axis runs over, the one named last changes fastest.
Arguments:
- activation_grams: float32 [2, 7168, 7168], P('task', 'row'), may hold values from -240 to 240, as said below
- adjusted_weights: bfloat16 [2, 7168, 2048], P('task', 'row'), may hold values from -0.59765625 to 0.59765625
Outputs:
- reduced_gram: float32 [7168, 7168], P('row')
- reduced_rhs: float32 [7168, 2048], P('row')
Inputs may be any that keep to these rules, and one draw needn't show every extreme that they name: Each activation_grams[m] is symmetric and positive definite.
All inputs are finite; a program needn't handle non-finite values.
Results may differ from a plain program's by a relative error of at most 0.0003.
Values may be sent and summed in bfloat16 or wider, within the bound.
A program may use at most 128 MiB of HBM per device.

v0:
```python
import functools

import jax
import jax.numpy as jnp
from jax import lax
from jax.sharding import Mesh
from jax.sharding import PartitionSpec as P

PANEL_STEPS = 2
ROW = ("row_0", "row_1", "row_2")


def over_axes(array, axes):
    return functools.reduce(lax.psum, axes, array)


def gathered_total(array, axis):
    return lax.all_gather(array, axis).sum(0)


def broadcast(value, axis, source):
    kept = jnp.where(lax.axis_index(axis) == source, value, 0).astype(value.dtype)
    return lax.psum(kept, axis)


def product(left, right):
    return jnp.dot(left, right, precision=lax.Precision.HIGHEST)


def per_device(activation_grams, adjusted_weights):
    local_models, rows, width = activation_grams.shape
    columns = adjusted_weights.shape[2]
    position = lax.axis_index(ROW)
    start_col = position * rows
    own_block = lax.dynamic_slice_in_dim(activation_grams, start_col, rows, 2)
    diagonal_entries = jnp.diagonal(own_block, axis1=1, axis2=2)
    total_trace = over_axes(jnp.sum(diagonal_entries, axis=1), ROW)
    scaling = width / total_trace
    identity_block = jnp.eye(rows, dtype=jnp.float32)
    new_block = 0.9 * own_block + 0.1 * (diagonal_entries[:, :, None] * identity_block)
    regular = lax.dynamic_update_slice_in_dim(0.9 * activation_grams, new_block, start_col, 2)
    source = scaling[:, None, None] * regular
    form = "mbn,mnd->bd"
    initial = jnp.zeros((rows, columns), jnp.float32)
    piece = lax.all_gather(adjusted_weights, ROW, axis=1, tiled=True)
    chosen = lax.slice_in_dim(source, 0, piece.shape[1], axis=2)
    folded = initial + jnp.einsum(
        form, chosen, piece.astype(jnp.float32), precision=lax.Precision.HIGHEST
    )
    merged_part = jnp.sum(source, axis=0)
    merged_rows, rhs_rows = (gathered_total(merged_part, "task"), gathered_total(folded, "task"))
    for panel in range(PANEL_STEPS):
        diag_block = lax.dynamic_slice_in_dim(merged_rows, start_col, rows, 1)
        diag_block = jnp.where(position >= panel, diag_block, identity_block)
        factor = jnp.linalg.cholesky(diag_block)
        upper_rows = jax.scipy.linalg.solve_triangular(factor, merged_rows, lower=True)
        solved_rows = jax.scipy.linalg.solve_triangular(factor, rhs_rows, lower=True)
        upper_rows, solved_rows = (
            broadcast(upper_rows, ROW, panel),
            broadcast(solved_rows, ROW, panel),
        )
        mine = lax.dynamic_slice_in_dim(upper_rows, start_col, rows, 1).T
        merged_next = merged_rows - product(mine, upper_rows)
        rhs_next = rhs_rows - product(mine, solved_rows)
        merged_rows = jnp.where(
            position == panel, upper_rows, jnp.where(position > panel, merged_next, merged_rows)
        )
        rhs_rows = jnp.where(
            position == panel, solved_rows, jnp.where(position > panel, rhs_next, rhs_rows)
        )
    return (merged_rows, rhs_rows)


def solution(mesh):
    torus = Mesh(
        mesh.devices.reshape(mesh.shape["task"], 4, 4, 4), ("task", "row_0", "row_1", "row_2")
    )
    in_specs = (P("task", ROW, None), P("task", ROW, None))
    out_specs = (P(ROW, None), P(ROW, None))
    return jax.shard_map(
        per_device, mesh=torus, in_specs=in_specs, out_specs=out_specs, check_vma=False
    )
```

profile of v0, /device:TPU:1, one launch (start us, length us, event | category | flops | bytes accessed | tf_op | source)
XLA Modules:
  0.0 562.2 jit_solution(3020141318296678471)
XLA Ops:
  7.2 0.0 all-gather.7.cloned.1.call-start
  7.2 0.7 all-gather.7.cloned.1.call-update
  7.9 0.0 all-gather.5.cloned.1.call-start
  8.0 1.0 dynamic-slice_bitcast_fusion
  9.0 1.7 gather_fusion
  10.6 0.6 reduce_sum.33
  11.3 9.9 %psum.49 = f32[1]{0:T(128)} all-reduce(f32[1]{0:T(128)} %bitcast.2), channel_id=1, replica_groups=mesh['task'=2,'row_0'=4,'row_1'=4,'row_2'=4] {'row_0'}, use_global_device_ids=true, to_apply=%region_1.2 | all-reduce | flops 1 | bytes 8 | tf_op jit(solution)/shard_map/psum | solution.py:14
  21.1 9.7 %psum.50 = f32[1]{0:T(128)} all-reduce(f32[1]{0:T(128)} %psum.49), channel_id=1, replica_groups=mesh['task'=2,'row_0'=4,'row_1'=4,'row_2'=4] {'row_1'}, use_global_device_ids=true, to_apply=%region_2.3 | all-reduce | flops 1 | bytes 8 | tf_op jit(solution)/shard_map/psum | solution.py:14
  30.9 10.7 %psum.51 = f32[1]{0:T(128)} all-reduce(f32[1]{0:T(128)} %psum.50), channel_id=1, replica_groups=mesh['task'=2,'row_0'=4,'row_1'=4,'row_2'=4] {'row_2'}, use_global_device_ids=true, to_apply=%region_3.4 | all-reduce | flops 1 | bytes 8 | tf_op jit(solution)/shard_map/psum | solution.py:14
  42.2 1.0 multiply_add_fusion
  43.3 2.2 broadcast_multiply_fusion
  45.5 0.6 dynamic_update_slice.3
  46.1 2.0 broadcast_multiply_fusion.1
  48.0 0.0 all-gather.5.cloned.1.call-update
  48.1 0.0 all-gather.9.cloned.1.call-start
  48.1 112.0 %all-gather.7.cloned.1.call-done = bf16[1,7168,2048]{2,1,0:T(8,128)(2,1)} async-done(((bf16[1,112,2048]{2,1,0:T(8,128)(2,1)}), bf16[1,7168,2048]{2,1,0:T(8,128)(2,1)}) %all-gather.7.cloned.1.call-update) | async-done | bytes 29360144 | tf_op jit(solution)/shard_map/all_gather | solution.py:45
  160.1 17.1 %fusion = f32[112,2048]{1,0:T(8,128)} fusion(bf16[1,7168,2048]{2,1,0:T(8,128)(2,1)} %all-gather.7.cloned.1.call-done, f32[1,112,7168]{2,1,0:T(8,128)S(1)} %copy-done.1), kind=kOutput, calls=%fused_computation.1 | convolution fusion | flops 19730006016 | bytes 33488896 | tf_op jit(solution)/shard_map/mbn,mnd->bd/dot_general | solution.py:47
  177.3 0.0 all-reduce.7.cloned.1.call-start
  177.3 4.9 all-gather.5.cloned.1.call-done
  182.2 3.6 reduce_sum.35
  185.8 3.1 copy.18
  188.9 0.8 convert_select_fusion.1
  189.7 0.1 copy.19
  189.8 0.8 fusion.18
  190.7 10.2 %cholesky.44 = f32[112,112]{1,0:T(8,128)S(1)} custom-call(f32[112,112]{1,0:T(8,128)S(1)} %fusion.18), custom_call_target="Cholesky" | custom-call | tf_op jit(solution)/shard_map/jit(cholesky)/cholesky | solution.py:55
  201.0 0.6 compare_reduce_fusion.1
  201.6 0.7 fusion.11
  202.3 8.6 %custom-call.12 = f32[1,112,112]{1,2,0:T(8,128)S(1)} custom-call(f32[1,112,112]{2,1,0:T(8,128)S(1)} %fusion.11), custom_call_target="InvertDiagBlocksLowerTriangular" | custom-call | tf_op jit(solution)/shard_map/jit(_solve_triangular)/triangular_solve | solution.py:56
  210.8 7.8 %convolution_select_fusion.1 = f32[112,7168]{0,1:T(8,128)} fusion(f32[112,7168]{1,0:T(8,128)S(1)} %reduce_sum.35, pred[]{:T(512)S(6)} %eq.27, f32[1,112,112]{1,2,0:T(8,128)S(1)} %custom-call.12), kind=kOutput, calls=%fused_computation.10 | convolution fusion | flops 1079787520 | bytes 6472705 | tf_op jit(solution)/shard_map/jit(_solve_triangular)/triangular_solve | solution.py:56
  218.6 1.7 reduce_sum.36
  220.4 1.9 convolution_select_fusion.3
  222.2 0.2 all-reduce.7.cloned.1.call-update
  222.5 0.0 all-reduce.5.cloned.1.call-start
  222.5 140.6 %all-reduce.7.cloned.1.call-done = (f32[112,7168]{0,1:T(8,128)}, f32[112,2048]{1,0:T(8,128)}) async-done(((f32[112,7168]{0,1:T(8,128)}, f32[112,2048]{1,0:T(8,128)}), (f32[112,7168]{0,1:T(8,128)}, f32[112,2048]{1,0:T(8,128)})) %all-reduce.7.cloned.1.call-update) | async-done | bytes 4128784 | tf_op jit(solution)/shard_map/psum | solution.py:23
  363.1 7.5 %fusion.5 = f32[112,7168]{0,1:T(8,128)S(1)} fusion(f32[112,7168]{0,1:T(8,128)} %get-tuple-element.13, f32[112,7168]{0,1:T(8,128)} %copy.18, pred[]{:T(512)S(6)} %gt.8, pred[]{:T(512)S(6)} %eq.27, s32[]{:T(128)S(6)} %select_n.105), kind=kOutput, calls=%fused_computation.9 | convolution fusion | flops 1081393152 | bytes 14278662 | tf_op jit(solution)/shard_map/dot_general | solution.py:27
  370.6 1.8 fusion.10
  372.5 0.1 copy.24
  372.6 0.8 fusion.15
  373.4 10.2 %cholesky.55 = f32[112,112]{1,0:T(8,128)S(1)} custom-call(f32[112,112]{1,0:T(8,128)S(1)} %fusion.15), custom_call_target="Cholesky" | custom-call | tf_op jit(solution)/shard_map/jit(cholesky)/cholesky | solution.py:55
  383.7 0.6 compare_reduce_fusion
  384.3 0.7 fusion.12
  385.0 8.6 %custom-call.13 = f32[1,112,112]{1,2,0:T(8,128)S(1)} custom-call(f32[1,112,112]{2,1,0:T(8,128)S(1)} %fusion.12), custom_call_target="InvertDiagBlocksLowerTriangular" | custom-call | tf_op jit(solution)/shard_map/jit(_solve_triangular)/triangular_solve | solution.py:56
  393.6 5.9 %convolution_select_fusion = f32[112,7168]{0,1:T(8,128)} fusion(f32[112,7168]{0,1:T(8,128)} %copy-done, pred[]{:T(512)S(6)} %eq.26, f32[1,112,112]{1,2,0:T(8,128)S(1)} %custom-call.13), kind=kOutput, calls=%fused_computation.6 | convolution fusion | flops 1079787520 | bytes 6472705 | tf_op jit(solution)/shard_map/jit(_solve_triangular)/triangular_solve | solution.py:56
  399.5 1.9 convolution_select_fusion.2
  401.4 137.7 %all-reduce.5.cloned.1.call-done = (f32[112,7168]{0,1:T(8,128)}, f32[112,2048]{1,0:T(8,128)}) async-done(((f32[112,7168]{0,1:T(8,128)}, f32[112,2048]{1,0:T(8,128)}), (f32[112,7168]{0,1:T(8,128)}, f32[112,2048]{1,0:T(8,128)})) %all-reduce.5.cloned.1.call-update) | async-done | bytes 4128784 | tf_op jit(solution)/shard_map/psum | solution.py:23
  539.2 8.7 %fusion.3 = f32[112,7168]{0,1:T(8,128)} fusion(f32[112,7168]{0,1:T(8,128)} %get-tuple-element.11, f32[112,7168]{0,1:T(8,128)} %copy-done, pred[]{:T(512)S(6)} %gt.9, pred[]{:T(512)S(6)} %eq.26, s32[]{:T(128)S(6)} %select_n.105), kind=kOutput, calls=%fused_computation.5 | convolution fusion | flops 1081393152 | bytes 14278662 | tf_op jit(solution)/shard_map/dot_general | solution.py:27
  547.9 2.7 fusion.8
  550.5 5.1 copy.27
  (15 shorter events, 0.1 us)
Async XLA Ops:
  7.2 152.9 %all-gather.7.cloned.1.call-start = ((), (), s32[]{:S(2)}) async-start(), calls=%async_computation.1 | async-start | bytes 29818880 | tf_op jit(solution)/shard_map/all_gather | solution.py:45
  7.9 174.3 %all-gather.5.cloned.1.call-start = ((), (), s32[]{:S(2)}) async-start(), calls=%async_computation | async-start | bytes 9633792 | tf_op jit(solution)/shard_map/all_gather | solution.py:18
  48.0 112.1 %copy-start.1 = (f32[1,112,7168]{2,1,0:T(8,128)S(1)}, f32[1,112,7168]{2,1,0:T(8,128)}, u32[]{:S(2)}) copy-start(f32[1,112,7168]{2,1,0:T(8,128)} %broadcast_multiply_fusion.1) | copy-start | bytes 9633796
  48.1 170.6 %all-gather.9.cloned.1.call-start = ((), (), s32[]{:S(2)}) async-start(), calls=%async_computation.2 | async-start | bytes 2752512 | tf_op jit(solution)/shard_map/all_gather | solution.py:18
  177.3 185.9 %all-reduce.7.cloned.1.call-start = ((), (), s32[]{:S(2)}) async-start(), calls=%async_computation.4 | async-start | bytes 9175040 | tf_op jit(solution)/shard_map/psum | solution.py:23
  222.5 316.7 %all-reduce.5.cloned.1.call-start = ((), (), s32[]{:S(2)}) async-start(), calls=%async_computation.3 | async-start | bytes 9175040 | tf_op jit(solution)/shard_map/psum | solution.py:23
  363.1 7.5 %copy-start.2 = (f32[112,2048]{1,0:T(8,128)S(1)}, f32[112,2048]{1,0:T(8,128)}, u32[]{:S(2)}) copy-start(f32[112,2048]{1,0:T(8,128)} %get-tuple-element.14) | copy-start | bytes 2752516
  370.6 1.8 copy-start
  539.2 8.7 %copy-start.3 = (f32[112,2048]{1,0:T(8,128)S(1)}, f32[112,2048]{1,0:T(8,128)}, u32[]{:S(2)}) copy-start(f32[112,2048]{1,0:T(8,128)} %get-tuple-element.12) | copy-start | bytes 2752516
Sparse Core Ops, SparseCore 0:
  10.8 149.2 all-gather.6
  162.3 19.8 all-gather.4
  184.4 14.2 all-gather.8
  222.6 140.4 all-reduce.6
  401.5 137.5 all-reduce.4
where the time goes:
time: 564 us; the launch traced here: 562 us
  waiting for transfers between devices  396 us (70%)
  matrix products  55.2 us (10%)
  other arithmetic  53.9 us (10%)
  blocking collectives  30.3 us (5%)
  between operations  14.7 us (3%)
  local copies, waits for them, and re-layouts  11.7 us (2%)
    psum x2, waiting for transfers between devices, broadcast(): return lax.psum(kept, axis)  278 us
    all_gather x1, waiting for transfers between devices, per_device(): piece = lax.all_gather(adjusted_weights, ROW, axis=1, tiled=True)  112 us
    psum x3, blocking collectives, over_axes(): return functools.reduce(lax.psum, axes, array)  30.3 us
    another operation x6, other arithmetic, per_device(): factor = jnp.linalg.cholesky(diag_block)  21.8 us
    dot_general x4, matrix products, product(): return jnp.dot(left, right, precision=lax.Precision.HIGHEST)  20.6 us
    another operation x4, other arithmetic, per_device(): jax.scipy.linalg.solve_triangular(factor, merged_rows, lower=True)  18.5 us
    dot_general x1, matrix products, per_device(): jnp.einsum(form, chosen, piece.astype(jnp.float32), precision=lax.Precisi...  17.1 us
    another operation x2, matrix products, per_device(): jax.scipy.linalg.solve_triangular(factor, merged_rows, lower=True)  13.7 us
  transfers between devices with their start and end apart: 5, of which 4 were waited for; matrix products, arithmetic and copies ran while one was open for 11% of the time, Pallas kernels for 0%

commit v1 on v0

v1 whole, which is shorter than its diff:
```python
import functools

import jax
import jax.numpy as jnp
from jax import lax
from jax.experimental import pallas as pl
from jax.experimental.pallas import tpu as pltpu
from jax.sharding import Mesh
from jax.sharding import PartitionSpec as P

ROW = ("row_0", "row_1", "row_2")
F32 = jnp.float32
BF16 = jnp.bfloat16
B = 112
T = 224
H = 7168
DC = 2048
KX = 1792
HALF = 3584
MESH = pl.DeviceIdType.MESH
HI = lax.Precision.HIGHEST
NCOPY = 176


class Net:
    def __init__(self, send, recv):
        self.send, self.recv, self.n, self.all = send, recv, 0, []

    def copy(self, src, dst, dev, track=True):
        i = self.n
        self.n += 1
        c = pltpu.make_async_remote_copy(
            src_ref=src, dst_ref=dst, send_sem=self.send.at[i], recv_sem=self.recv.at[i],
            device_id=dev, device_id_type=MESH)
        if track:
            self.all.append(c)
        return c

    def go(self, src, dst, dev):
        c = self.copy(src, dst, dev)
        c.start()
        return c


def iota(shape, dim):
    return lax.broadcasted_iota(jnp.int32, shape, dim)


def dot(a, b, dims=((1,), (0,)), precision=None):
    return lax.dot_general(a, b, (dims, ((), ())), precision=precision, preferred_element_type=F32)


def body(a_ref, w_ref, og_ref, or_ref,
         at, bnc, wg, rt, lh, ll, utx, ug, pbuf, prx, sb, rl, rr, rb, fin, finp,
         ah, ap, oh, g, linv, sx, sr, mx, mr, trx, try_, trz, trp, dw, q, send, recv, lsem):
    t = lax.axis_index("task")
    x, y, z = (lax.axis_index(n) for n in ROW)
    p = y * 4 + z
    r = x * 16 + p

    def add(v, d):
        return lax.rem(v + (4 + d), 4)

    def dev(dt=0, dx=0, dy=0, dz=0):
        return (1 - t if dt else t, add(x, dx) if dx else x, add(y, dy) if dy else y, add(z, dz) if dz else z)

    net = Net(send, recv)
    bar = pltpu.get_barrier_semaphore()
    peers = [dev(dt=1)] + [dev(**{a: d}) for a in ("dx", "dy", "dz") for d in (1, -1, 2)]
    for d in peers:
        pl.semaphore_signal(bar, inc=1, device_id=d, device_id_type=MESH)
    pl.semaphore_wait(bar, len(peers))

    ws = (r * 7 // 8 - r // 63) * 128
    ws = pl.multiple_of(ws, 128)
    l_rt = pltpu.make_async_copy(a_ref.at[0, :, 0:256], rt.at[y, z], lsem.at[0])
    l_dw = pltpu.make_async_copy(a_ref.at[0, :, pl.ds(ws, 256)], dw, lsem.at[1])
    l_w = pltpu.make_async_copy(w_ref.at[0], wg.at[y, z], lsem.at[2])
    kx = pl.multiple_of(x * KX, 128)
    l_at = pltpu.make_async_copy(a_ref.at[0, :, pl.ds(kx, KX)], at.at[x], lsem.at[3])
    hc = pl.multiple_of(t * HALF, 128)
    hp = pl.multiple_of((1 - t) * HALF, 128)
    l_ah = pltpu.make_async_copy(a_ref.at[0, :, pl.ds(hc, HALF)], ah, lsem.at[4])
    for c in (l_rt, l_dw, l_w, l_at, l_ah):
        c.start()

    def acol(d):
        return pl.ds(pl.multiple_of(add(x, d) * KX, 128), KX)

    xb = [net.go(a_ref.at[0, 0:56, acol(2)], bnc.at[0], dev(dx=1)),
          net.go(a_ref.at[0, 56:112, acol(2)], bnc.at[1], dev(dx=-1))]
    xd = [net.go(a_ref.at[0, :, acol(1)], at.at[x], dev(dx=1)),
          net.go(a_ref.at[0, :, acol(-1)], at.at[x], dev(dx=-1))]
    xp = net.go(a_ref.at[0, :, pl.ds(hp, HALF)], ap, dev(dt=1))

    def gather(sl, batch):
        def nb(h, stage, d):
            axis = ("dy", "dz")[(h + stage) % 2]
            return dev(**{axis: d})

        def ref(h, part, a, b):
            return sl(h, part, a, b) if h == 0 else sl(h, part, b, a)

        first, second = (y, z), (z, y)
        st = {}

        def ph1(h):
            s = ref(h, None, first[h], second[h])
            st[h, "p"] = net.go(s, s, nb(h, 0, 1))
            st[h, "m"] = net.go(s, s, nb(h, 0, -1))

        def ph2(h, k, a):
            s = ref(h, None, a, second[h])
            st[h, k, "p"] = net.go(s, s, nb(h, 1, 1))
            st[h, k, "m"] = net.go(s, s, nb(h, 1, -1))

        def fw1(h, side):
            d = -1 if side == "p" else 1
            st[h, side].wait_recv()
            s = ref(h, 0 if side == "p" else 1, add(first[h], d), second[h])
            st[h, "f" + side] = net.go(s, s, nb(h, 0, -d))

        def end1(h):
            st[h, "fp"].wait_recv()
            st[h, "fm"].wait_recv()

        def fw2(h, k, a, side):
            d = -1 if side == "p" else 1
            st[h, k, side].wait_recv()
            s = ref(h, 0 if side == "p" else 1, a, add(second[h], d))
            st[h, k, "f" + side] = net.go(s, s, nb(h, 1, -d))

        def end2(h, k):
            st[h, k, "fp"].wait_recv()
            st[h, k, "fm"].wait_recv()

        ev = []
        both = (0, 1)
        if batch:
            every = slice(None)
            ev.append(lambda: [ph1(h) for h in both])
            for side in "pm":
                for h in both:
                    ev.append(functools.partial(fw1, h, side))
            ev.append(lambda: [(end1(h), ph2(h, 0, every)) for h in both])
            for side in "pm":
                for h in both:
                    ev.append(functools.partial(fw2, h, 0, every, side))
            ev.append(lambda: [end2(h, 0) for h in both])
            return ev
        idx = {k: (lambda h, d=d: add(first[h], d) if d else first[h]) for k, d in ((0, 0), (1, -1), (2, 1), (3, 2))}
        ev.append(lambda: ([ph1(h) for h in both], [ph2(h, 0, first[h]) for h in both]))
        for k, side in ((1, "p"), (2, "m")):
            for h in both:
                ev.append(lambda h=h, k=k, side=side: (fw1(h, side), ph2(h, k, idx[k](h))))
        for h in both:
            for side in "pm":
                ev.append(lambda h=h, side=side: fw2(h, 0, idx[0](h), side))
        for h in both:
            ev.append(lambda h=h: (end1(h), ph2(h, 3, idx[3](h))))
        for k in (1, 2, 3):
            for h in both:
                for side in "pm":
                    ev.append(lambda h=h, k=k, side=side: fw2(h, k, idx[k](h), side))
        ev.append(lambda: [end2(h, k) for k in range(4) for h in both])
        return ev

    def sl_rt(h, part, a, b):
        rows = slice(None) if part is None else pl.ds(56 * part, 56)
        return rt.at[a, b, rows, pl.ds(128 * h, 128)]

    def sl_w(h, part, a, b):
        lo, n = (1024 * h, 1024) if part is None else (1024 * h + 512 * part, 512)
        return wg.at[a, b, :, pl.ds(lo, n)]

    def sl_u(h, part, a, b):
        blk = slice(None) if part is None else part
        return ug.at[blk, a, b, :, pl.ds(128 * h, 128)]

    ev_r = gather(sl_rt, True)
    ev_w = gather(sl_w, False)
    ev_u = gather(sl_u, False)

    def pump(ev, n=1):
        for _ in range(min(n, len(ev))):
            ev.pop(0)()

    l_rt.wait()
    pump(ev_r)

    l_dw.wait()
    off = r * B - ws
    tile = iota((B, 256), 1) == iota((B, 256), 0) + off
    part = jnp.sum(jnp.where(tile, dw[...], 0.0), axis=1, keepdims=True)
    part = jnp.sum(part, axis=0, keepdims=True)

    def spread(buf, val, pos, axis):
        buf[pos] = jnp.broadcast_to(val, (8, 128))
        return [net.go(buf.at[pos], buf.at[pos], dev(**{axis: d})) for d in (1, -1, 2)]

    def total(buf, copies):
        for c in copies:
            c.wait_recv()
        return buf[0] + buf[1] + (buf[2] + buf[3])

    cs = spread(trx, part, x, "dx")
    s = total(trx, cs)
    cs = spread(try_, s, y, "dy")
    pump(ev_r, 4)
    s = total(try_, cs)
    cs = spread(trz, s, z, "dz")
    l_w.wait()
    pump(ev_r, 1)
    s = total(trz, cs)
    scale8 = float(H) / s
    trp[0] = scale8
    cp = net.go(trp.at[0], trp.at[1], dev(dt=1))
    pump(ev_r, 4)
    pump(ev_w, 1)
    pump(ev_r, 1)
    scale = scale8[0:1, 0:1]

    lane = iota((B, 256), 1)
    own = rt[y, z]
    hit = lane == iota((B, 256), 0) + r * B
    own = jnp.where(lane < T, own * jnp.where(hit, scale, 0.9 * scale), 0.0)
    mx[...] = own
    cm = net.go(mx, mr, dev(dt=1))
    for i in range(2):
        hit = lane == iota((B, 256), 0) + i * B
        sx[i] = jnp.where(lane < T, rt[0, i] * jnp.where(hit, scale, 0.9 * scale), 0.0)
    cS = net.go(sx, sr, dev(dt=1))
    cp.wait_recv()
    scale_p = trp[1][0:1, 0:1]
    cm.wait_recv()
    cS.wait_recv()

    def chol_steps():
        def start():
            linv[T:256, :] = jnp.zeros((256 - T, 256), F32)
            for i in range(2):
                g[B * i:B * (i + 1), 0:256] = sx[i] + sr[i]
            g[:, 256:512] = jnp.where(iota((T, 256), 0) == iota((T, 256), 1), 1.0, 0.0)

        def step(b):
            k0 = 16 * b
            rr_ = g[k0:k0 + 16, :]
            rid = iota((16, 1), 0)
            for j in range(16):
                row = rr_[j:j + 1, :]
                col = rr_[:, k0 + j:k0 + j + 1]
                inv = 1.0 / row[:, k0 + j:k0 + j + 1]
                rr_ = rr_ - jnp.where(rid > j, col * inv, 0.0) * row
            dg = jnp.sum(jnp.where(iota((16, 512), 1) == iota((16, 512), 0) + k0, rr_, 0.0), axis=1, keepdims=True)
            rr_ = rr_ * (1.0 / jnp.sqrt(dg))
            linv[k0:k0 + 16, :] = rr_[:, 256:512]
            if b < 13:
                left = jnp.where(iota((16, 256), 1) >= k0 + 16, rr_[:, 0:256], 0.0)
                upd = dot(left, rr_, ((0,), (0,)), HI)
                g[k0 + 16:T, :] = g[k0 + 16:T, :] - upd[k0 + 16:T, :]

        return [start] + [functools.partial(step, b) for b in range(14)]

    for f in chol_steps():
        pl.when(x == 0)(f)
        pump(ev_w, 1)
    lc = [net.copy(linv, linv, dev(dx=d), track=False) for d in (1, 2, -1)]

    @pl.when(x == 0)
    def _():
        for c in lc:
            c.start()
        for c in lc:
            c.wait_send()

    for i, c in enumerate(lc):
        @pl.when(x == (1, 2, 3)[i])
        def _(c=c):
            c.wait_recv()

    ut = dot(mx[...] + mr[...], linv[...], ((1,), (1,)), HI)
    utx[x] = ut
    cu = [net.go(utx.at[x], utx.at[x], dev(dx=d)) for d in (1, -1, 2)]
    pump(ev_w, 2)
    xb[0].wait_recv()
    f0 = net.go(bnc.at[0], at.at[add(x, -1), 0:56], dev(dx=1))
    xb[1].wait_recv()
    f1 = net.go(bnc.at[1], at.at[add(x, 1), 56:112], dev(dx=-1))
    for c in cu:
        c.wait_recv()
    for i in range(2):
        ug[i, y, z] = utx[2 * t + i]
    pump(ev_u, 1)
    pump(ev_w, 99)
    for c in xd + [f0, f1]:
        c.wait_recv()
    l_at.wait()

    def split(v):
        hi = v.astype(BF16)
        return hi, (v - hi.astype(F32)).astype(BF16)

    for i in range(4):
        v = at[i]
        same = (i == x).astype(jnp.int32)
        hit = iota((B, KX), 1) == iota((B, KX), 0) + (p * B + (1 - same) * H)
        v = v * jnp.where(hit, 1.0, 0.9)
        lh[B * i:B * (i + 1), :], ll[B * i:B * (i + 1), :] = split(v)
    v = rt[...].reshape(KX, 256)
    hit = iota((KX, 256), 0) + x * KX == iota((KX, 256), 1)
    v = jnp.where(iota((KX, 256), 1) < T, v * jnp.where(hit, 1.0, 0.9), 0.0)
    v = v.T
    lh[448:704, :], ll[448:704, :] = split(v)

    top = (p < 2).astype(F32)
    sel = jnp.where(iota((B, 256), 1) == iota((B, 256), 0) + p * B, -1.0, 0.0)
    q[0] = utx[0] * (1.0 - top) + sel * top
    for i in range(1, 4):
        q[i] = utx[i]

    cd = []
    for j in range(8):
        n = lax.rem((1 - t) * 4 + j, 8)
        wcol = wg[:, :, :, pl.ds(pl.multiple_of(n * 256, 256), 256)].reshape(KX, 256)
        acc = dot(lh[...], wcol) + dot(ll[...], wcol)
        yv = dot(linv[...], acc[448:704], precision=HI)
        cor = dot(q[...].reshape(448, 256), yv, precision=HI)
        for i in range(4):
            pc = acc[B * i:B * (i + 1)]
            if i == 0:
                pc = pc * (1.0 - top)
            pbuf[j, i] = (pc - cor[B * i:B * (i + 1)]) * scale
        if j < 4:
            cd.append(net.go(pbuf.at[j], prx.at[j], dev(dt=1)))
        pump(ev_u, 3)
    for j in range(4):
        cd[j].wait_recv()
        for i in range(4):
            sb[i, j] = pbuf[4 + j, i] + prx[j, i]

    o = add(x, 2)
    r0 = net.go(sb.at[o, 0:2], rl, dev(dx=1))
    r1 = net.go(sb.at[o, 2:4], rr, dev(dx=-1))
    r0.wait_recv()
    xn = add(x, 1)
    sb[xn, 0:2] = sb[xn, 0:2] + rl[...]
    r2 = net.go(sb.at[xn], rb.at[0], dev(dx=1))
    r1.wait_recv()
    xm = add(x, -1)
    sb[xm, 2:4] = sb[xm, 2:4] + rr[...]
    r3 = net.go(sb.at[xm], rb.at[1], dev(dx=-1))
    pump(ev_u, 99)

    l_ah.wait()
    xp.wait_recv()
    topr = (r < 2).astype(F32)
    selr = jnp.where(iota((B, 256), 1) == iota((B, 256), 0) + r * B, -1.0, 0.0)
    qc = utx[x] * (1.0 - topr) + selr * topr
    keep = 1.0 - topr
    lcp = []
    for i in range(2):
        for c in range(7):
            cc = i * 7 + c
            cols = slice(cc * 256, (cc + 1) * 256)
            u = ug[i].reshape(KX, 256)[c * 256:(c + 1) * 256]
            hit = iota((B, 256), 1) + (cc * 256) == iota((B, 256), 0) + (r * B - t * HALF)
            m = ah[:, cols] * (scale * keep) + ap[:, cols] * (scale_p * keep)
            oh[:, cols] = m * jnp.where(hit, 1.0, 0.9) - dot(qc, u, ((1,), (1,)), HI)
    co = pltpu.make_async_copy(oh, og_ref.at[:, pl.ds(hc, HALF)], lsem.at[5])
    co.start()
    cg = net.go(oh, og_ref.at[:, pl.ds(hc, HALF)], dev(dt=1))

    r2.wait_recv()
    r3.wait_recv()
    fin[...] = sb[x] + (rb[0] + rb[1])
    cf = net.go(fin, finp, dev(dt=1))
    cf.wait_recv()
    for j in range(4):
        or_ref[:, pl.ds(pl.multiple_of(t * 1024 + 256 * j, 256), 256)] = fin[j]
        or_ref[:, pl.ds(pl.multiple_of((1 - t) * 1024 + 256 * j, 256), 256)] = finp[j]
    co.wait()
    cg.wait_recv()
    for c in net.all:
        c.wait_send()
    assert net.n <= NCOPY, net.n


def per_device(grams, weights):
    V = pltpu.VMEM
    scratch = [
        V((4, B, KX), F32), V((2, 56, KX), F32), V((4, 4, B, DC), BF16), V((4, 4, B, 256), F32),
        V((704, KX), BF16), V((704, KX), BF16), V((4, B, 256), F32), V((2, 4, 4, B, 256), F32),
        V((8, 4, B, 256), F32), V((4, 4, B, 256), F32), V((4, 4, B, 256), F32),
        V((2, B, 256), F32), V((2, B, 256), F32), V((2, 4, B, 256), F32), V((4, B, 256), F32), V((4, B, 256), F32),
        V((B, HALF), F32), V((B, HALF), F32), V((B, HALF), F32), V((T, 512), F32), V((256, 256), F32),
        V((2, B, 256), F32), V((2, B, 256), F32), V((B, 256), F32), V((B, 256), F32),
        V((4, 8, 128), F32), V((4, 8, 128), F32), V((4, 8, 128), F32), V((2, 8, 128), F32),
        V((B, 256), F32), V((4, B, 256), F32),
        pltpu.SemaphoreType.DMA((NCOPY,)), pltpu.SemaphoreType.DMA((NCOPY,)), pltpu.SemaphoreType.DMA((8,)),
    ]
    return pl.pallas_call(
        body,
        out_shape=(jax.ShapeDtypeStruct((B, H), F32), jax.ShapeDtypeStruct((B, DC), F32)),
        in_specs=[pl.BlockSpec(memory_space=pl.ANY)] * 2,
        out_specs=(pl.BlockSpec(memory_space=pl.ANY), pl.BlockSpec(memory_space=pltpu.VMEM)),
        scratch_shapes=scratch,
        compiler_params=pltpu.CompilerParams(
            collective_id=0, has_side_effects=True, vmem_limit_bytes=62 * 1024 * 1024),
    )(grams, weights)


def solution(mesh):
    torus = Mesh(mesh.devices.reshape(mesh.shape["task"], 4, 4, 4), ("task",) + ROW)
    return jax.shard_map(
        per_device, mesh=torus, in_specs=(P("task", ROW, None), P("task", ROW, None)),
        out_specs=(P(ROW, None), P(ROW, None)), check_vma=False)
```

time: 564 us -> 173 us (0.31)
  waiting for transfers between devices: 396 us -> 0 us
  Pallas kernels: 0 us -> 168 us
  matrix products: 55.2 us -> 0 us
  other arithmetic: 53.9 us -> 0 us
  blocking collectives: 30.3 us -> 0 us
  between operations: 14.7 us -> 0.65 us
  local copies, waits for them, and re-layouts: 11.7 us -> 4.86 us
    psum x2 -> x0, waiting for transfers between devices: 278 us -> none  [broadcast(): return lax.psum(kept, axis)]
    pallas_call x0 -> x1, Pallas kernels: none -> 168 us  [per_device(): pl.pallas_call(body, out_shape=(jax.ShapeDtypeStruct((B, H), F32), jax.Sh...]
    all_gather x3 -> x0, waiting for transfers between devices: 117 us -> none  [the longest x1 112 us: per_device(): piece = lax.all_gather(adjusted_weights, ROW, axis=1, tiled=True)]
    another operation x10 -> x0, other arithmetic: 40.3 us -> none  [the longest x6 21.8 us: per_device(): factor = jnp.linalg.cholesky(diag_block)]
    dot_general x5 -> x0, matrix products: 37.7 us -> none  [the longest x4 20.6 us: product(): return jnp.dot(left, right, precision=lax.Precision.HIGHEST)]
    psum x3 -> x0, blocking collectives: 30.3 us -> none  [over_axes(): return functools.reduce(lax.psum, axes, array)]
    another operation x4 -> x0, matrix products: 17.5 us -> none  [the longest x2 13.7 us: per_device(): jax.scipy.linalg.solve_triangular(factor, merged_rows, lower=True)]
    reduce_sum x3 -> x0, other arithmetic: 5.89 us -> none  [the longest x2 5.29 us: gathered_total(): return lax.all_gather(array, axis).sum(0)]
  transfers between devices with their start and end apart: 5 -> 0, of which waited for: 4 -> 0; matrix products, arithmetic and copies ran while one was open for 11% -> 0% of each run, Pallas kernels for 0% -> 0%
where the time goes in v1:
time: 173 us
  Pallas kernels  168 us (97%)
  local copies, waits for them, and re-layouts  4.86 us (3%)
    pallas_call x1, Pallas kernels, per_device(): pl.pallas_call(body, out_shape=(jax.ShapeDtypeStruct((B, H), F32), jax.Sh...  168 us
    unnamed x4, local copies, waits for them, and re-layouts  4.86 us

profile of v1, /device:TPU:1, one launch (start us, length us, event | category | flops | bytes accessed | tf_op | source)
XLA Modules:
  0.0 173.3 jit_solution(12396898653243741739)
XLA Ops:
  0.6 167.8 %shard_map.41 = (f32[112,7168]{1,0:T(8,128)}, f32[112,2048]{1,0:T(8,128)}) custom-call(f32[1,112,7168]{2,1,0:T(8,128)} %a_ref.1, bf16[1,112,2048]{2,1,0:T(8,128)(2,1)} %w_ref.1), custom_call_target="tpu_custom_call" | custom-call | tf_op jit(solution)/shard_map/pallas_call | solution.py:401
  168.4 0.0 copy-start
  168.4 3.9 %copy.6 = f32[112,7168]{1,0:T(8,128)} copy(f32[112,7168]{1,0:T(8,128)} %get-tuple-element.4) | data formatting | bytes 6422528
  172.3 0.0 copy-done
  172.4 0.9 copy.7
Async XLA Ops:
  168.4 4.0 %copy-start = (f32[112,2048]{1,0:T(8,128)S(1)}, f32[112,2048]{1,0:T(8,128)}, u32[]{:S(2)}) copy-start(f32[112,2048]{1,0:T(8,128)} %get-tuple-element.5) | copy-start | bytes 2752516

commit v2 on v1

v2 whole, which is shorter than its diff:
```python
import functools

import jax
import jax.numpy as jnp
from jax import lax
from jax.experimental import pallas as pl
from jax.experimental.pallas import tpu as pltpu
from jax.sharding import Mesh
from jax.sharding import PartitionSpec as P

ROW = ("row_0", "row_1", "row_2")
F32 = jnp.float32
BF16 = jnp.bfloat16
B = 112
T = 224
H = 7168
DC = 2048
KX = 1792
HALF = 3584
MESH = pl.DeviceIdType.MESH
HI = lax.Precision.HIGHEST
NCOPY = 208


class Net:
    def __init__(self, send, recv):
        self.send, self.recv, self.n, self.all = send, recv, 0, []

    def copy(self, src, dst, dev, track=True):
        i = self.n
        self.n += 1
        c = pltpu.make_async_remote_copy(
            src_ref=src, dst_ref=dst, send_sem=self.send.at[i], recv_sem=self.recv.at[i],
            device_id=dev, device_id_type=MESH)
        if track:
            self.all.append(c)
        return c

    def go(self, src, dst, dev):
        c = self.copy(src, dst, dev)
        c.start()
        return c


def iota(shape, dim):
    return lax.broadcasted_iota(jnp.int32, shape, dim)


def dot(a, b, dims=((1,), (0,)), precision=None):
    return lax.dot_general(a, b, (dims, ((), ())), precision=precision, preferred_element_type=F32)


def split(v):
    hi = v.astype(BF16)
    return hi, (v - hi.astype(F32)).astype(BF16)


def dot3(a, b, dims=((1,), (0,))):
    return dot(a[0], b[0], dims) + (dot(a[0], b[1], dims) + dot(a[1], b[0], dims))


def chol_steps(g, linv, corner):
    nb = 32

    def start():
        linv[T:256, 0:128] = jnp.zeros((256 - T, 128), F32)
        linv[T:256, 128:256] = jnp.zeros((256 - T, 128), F32)
        for i in range(2):
            g[B * i:B * (i + 1), 0:256] = corner(i)
        g[:, 256:512] = jnp.where(iota((T, 256), 0) == iota((T, 256), 1), 1.0, 0.0)

    def step(b):
        rid = iota((nb, 128), 0)
        k0 = nb * b
        left = [i for i in (0, 1) if 128 * (i + 1) > k0]
        tiles = left + [2] + ([3] if k0 + nb > 128 else [])
        v = {i: g[k0:k0 + nb, 128 * i:128 * i + 128] for i in tiles}

        def column(k):
            i = k // 128
            return jnp.broadcast_to(v[i][:, k % 128:k % 128 + 1], (nb, 128))

        for j in range(0, nb, 2):
            c0, c1 = column(k0 + j), column(k0 + j + 1)
            d00, d01, d11 = c0[j:j + 1], c1[j:j + 1], c1[j + 1:j + 2]
            inv = 1.0 / (d00 * d11 - d01 * d01)
            f0 = jnp.where(rid > j + 1, (d11 * inv) * c0 - (d01 * inv) * c1, 0.0)
            f1 = jnp.where(rid > j + 1, (d00 * inv) * c1 - (d01 * inv) * c0, 0.0)
            f0 = jnp.where(rid == j + 1, d01 / d00, f0)
            for i in tiles:
                v[i] = v[i] - f0 * v[i][j:j + 1, :] - f1 * v[i][j + 1:j + 2, :]
        dg = 0.0
        for i in left:
            dg = dg + jnp.sum(jnp.where(iota((nb, 128), 1) + 128 * i == rid + k0, v[i], 0.0), axis=1, keepdims=True)
        sc = 1.0 / jnp.sqrt(dg)
        for i in tiles:
            v[i] = v[i] * sc
        linv[k0:k0 + nb, 0:128] = v[2]
        if 3 in v:
            linv[k0:k0 + nb, 128:256] = v[3]
        if k0 + nb < T:
            lo = 128 if k0 + nb >= 128 else 0
            lhs = jnp.concatenate([v[i] for i in left if 128 * i >= lo], axis=1)
            off = k0 + nb - lo
            for i in tiles:
                if 128 * (i + 1) > lo:
                    cols = slice(128 * i, 128 * i + 128)
                    upd = dot(lhs, v[i], ((0,), (0,)), HI)
                    g[k0 + nb:T, cols] = g[k0 + nb:T, cols] - upd[off:off + T - k0 - nb, :]

    return [start] + [functools.partial(step, b) for b in range(T // nb)]


def body(a_ref, w_ref, og_ref, or_ref,
         at, bnc, wg, rt, lh, ll, mxx, q, ug, pbuf, prx, sb, rlr, rb, fin, finp,
         ah, ap, oh, g, linv, sx, sr, mx, mr, trx, try_, trz, trp, dw, send, recv, lsem):
    t = lax.axis_index("task")
    x, y, z = (lax.axis_index(n) for n in ROW)
    p = y * 4 + z
    r = x * 16 + p

    def add(v, d):
        return lax.rem(v + (4 + d), 4)

    def dev(dt=0, dx=0, dy=0, dz=0):
        return (1 - t if dt else t, add(x, dx) if dx else x, add(y, dy) if dy else y, add(z, dz) if dz else z)

    net = Net(send, recv)
    ws = pl.multiple_of((r * 7 // 8 - r // 63) * 128, 128)
    kx = pl.multiple_of(x * KX, 128)
    hc = pl.multiple_of(t * HALF, 128)
    hp = pl.multiple_of((1 - t) * HALF, 128)
    loads = [(a_ref.at[0, :, pl.ds(ws, 256)], dw), (a_ref.at[0, :, 0:256], rt.at[y, z]), (w_ref.at[0], wg.at[y, z]),
             (a_ref.at[0, :, pl.ds(kx, KX)], at.at[x]), (a_ref.at[0, :, pl.ds(hc, HALF)], ah)]
    loads = [pltpu.make_async_copy(a, b, lsem.at[i]) for i, (a, b) in enumerate(loads)]
    l_dw, l_rt, l_w, l_at, l_ah = loads
    for c in loads:
        c.start()
    bar = pltpu.get_barrier_semaphore()
    peers = [dev(dt=1)] + [dev(**{a: d}) for a in ("dx", "dy", "dz") for d in (1, -1, 2)]
    for d in peers:
        pl.semaphore_signal(bar, inc=1, device_id=d, device_id_type=MESH)
    pl.semaphore_wait(bar, len(peers))

    def spread(buf, val, pos, axis):
        buf[pos] = jnp.broadcast_to(val, (8, 128))
        return [net.go(buf.at[pos], buf.at[pos], dev(**{axis: d})) for d in (1, -1, 2)]

    def total(buf, copies):
        for c in copies:
            c.wait_recv()
        return buf[0] + buf[1] + (buf[2] + buf[3])

    def gather(sl, batch):
        def nb(h, stage, d):
            axis = ("dy", "dz")[(h + stage) % 2]
            return dev(**{axis: d})

        def ref(h, part, a, b):
            return sl(h, part, a, b) if h == 0 else sl(h, part, b, a)

        first, second = (y, z), (z, y)
        st = {}

        def ph1(h):
            s = ref(h, None, first[h], second[h])
            st[h, "p"] = net.go(s, s, nb(h, 0, 1))
            st[h, "m"] = net.go(s, s, nb(h, 0, -1))

        def ph2(h, k, a):
            s = ref(h, None, a, second[h])
            st[h, k, "p"] = net.go(s, s, nb(h, 1, 1))
            st[h, k, "m"] = net.go(s, s, nb(h, 1, -1))

        def fw1(h, side):
            d = -1 if side == "p" else 1
            st[h, side].wait_recv()
            s = ref(h, 0 if side == "p" else 1, add(first[h], d), second[h])
            st[h, "f" + side] = net.go(s, s, nb(h, 0, -d))

        def end1(h):
            st[h, "fp"].wait_recv()
            st[h, "fm"].wait_recv()

        def fw2(h, k, a, side):
            d = -1 if side == "p" else 1
            st[h, k, side].wait_recv()
            s = ref(h, 0 if side == "p" else 1, a, add(second[h], d))
            st[h, k, "f" + side] = net.go(s, s, nb(h, 1, -d))

        def end2(h, k):
            st[h, k, "fp"].wait_recv()
            st[h, k, "fm"].wait_recv()

        ev = []
        both = (0, 1)
        if batch:
            every = slice(None)
            ev.append(lambda: [ph1(h) for h in both])
            for side in "pm":
                for h in both:
                    ev.append(functools.partial(fw1, h, side))
            ev.append(lambda: [(end1(h), ph2(h, 0, every)) for h in both])
            for side in "pm":
                for h in both:
                    ev.append(functools.partial(fw2, h, 0, every, side))
            ev.append(lambda: [end2(h, 0) for h in both])
            return ev
        idx = {k: (lambda h, d=d: add(first[h], d) if d else first[h]) for k, d in ((0, 0), (1, -1), (2, 1), (3, 2))}
        ev.append(lambda: ([ph1(h) for h in both], [ph2(h, 0, first[h]) for h in both]))
        for k, side in ((1, "p"), (2, "m")):
            for h in both:
                ev.append(lambda h=h, k=k, side=side: (fw1(h, side), ph2(h, k, idx[k](h))))
        for h in both:
            for side in "pm":
                ev.append(lambda h=h, side=side: fw2(h, 0, idx[0](h), side))
        for h in both:
            ev.append(lambda h=h: (end1(h), ph2(h, 3, idx[3](h))))
        for k in (1, 2, 3):
            for h in both:
                for side in "pm":
                    ev.append(lambda h=h, k=k, side=side: fw2(h, k, idx[k](h), side))
        ev.append(lambda: [end2(h, k) for k in range(4) for h in both])
        return ev

    def sl_rt(h, part, a, b):
        rows = slice(None) if part is None else pl.ds(56 * part, 56)
        return rt.at[a, b, rows, pl.ds(128 * h, 128)]

    def sl_w(k, h, part, a, b):
        lo, n = (1024 * h + 512 * k, 512) if part is None else (1024 * h + 512 * k + 256 * part, 256)
        return wg.at[a, b, :, pl.ds(lo, n)]

    def sl_u(h, part, a, b):
        blk = slice(None) if part is None else part
        return ug.at[blk, a, b, :, pl.ds(128 * h, 128)]

    ev_r = gather(sl_rt, True)
    ev_w = [gather(functools.partial(sl_w, k), False) for k in range(2)]
    ev_u = gather(sl_u, False)

    def pump(ev, n=1):
        for _ in range(min(n, len(ev))):
            ev.pop(0)()

    l_rt.wait()
    pump(ev_r)
    l_dw.wait()
    tile = iota((B, 256), 1) == iota((B, 256), 0) + (r * B - ws)
    part = jnp.sum(jnp.where(tile, dw[...], 0.0), axis=1, keepdims=True)
    part = jnp.sum(part, axis=0, keepdims=True)
    cs = spread(trx, part, x, "dx")

    def acol(d):
        return pl.ds(pl.multiple_of(add(x, d) * KX, 128), KX)

    xb = [net.go(a_ref.at[0, 0:56, acol(2)], bnc.at[0], dev(dx=1)),
          net.go(a_ref.at[0, 56:112, acol(2)], bnc.at[1], dev(dx=-1))]
    xd = [net.go(a_ref.at[0, :, acol(1)], at.at[x], dev(dx=1)),
          net.go(a_ref.at[0, :, acol(-1)], at.at[x], dev(dx=-1))]
    xp = net.go(a_ref.at[0, :, pl.ds(hp, HALF)], ap, dev(dt=1))
    xf = []

    def relay0():
        xb[0].wait_recv()
        xf.append(net.go(bnc.at[0], at.at[add(x, -1), 0:56], dev(dx=1)))

    def relay1():
        xb[1].wait_recv()
        xf.append(net.go(bnc.at[1], at.at[add(x, 1), 56:112], dev(dx=-1)))

    ev_a = [relay0, relay1]

    s = total(trx, cs)
    cs = spread(try_, s, y, "dy")
    pump(ev_r, 4)
    s = total(try_, cs)
    cs = spread(trz, s, z, "dz")
    pump(ev_r, 1)
    s = total(trz, cs)
    scale8 = float(H) / s
    trp[0] = scale8
    cp = net.go(trp.at[0], trp.at[1], dev(dt=1))
    scale = scale8[0:1, 0:1]
    pump(ev_r, 4)
    l_w.wait()
    pump(ev_w[0], 1)
    pump(ev_r, 1)

    lane = iota((B, 256), 1)
    hit = lane == iota((B, 256), 0) + r * B
    mx[...] = jnp.where(lane < T, rt[y, z] * jnp.where(hit, scale, 0.9 * scale), 0.0)
    cm = net.go(mx, mr, dev(dt=1))
    for i in range(2):
        hit = lane == iota((B, 256), 0) + i * B
        sx[i] = jnp.where(lane < T, rt[0, i] * jnp.where(hit, scale, 0.9 * scale), 0.0)
    cS = net.go(sx, sr, dev(dt=1))
    cp.wait_recv()
    scale_p = trp[1][0:1, 0:1]
    cm.wait_recv()
    mxx[x] = mx[...] + mr[...]
    cu = [net.go(mxx.at[x], mxx.at[x], dev(dx=d)) for d in (1, -1, 2)]
    pump(ev_a, 2)
    cS.wait_recv()

    for f in chol_steps(g, linv, lambda i: sx[i] + sr[i]):
        pl.when(x == 0)(f)
        pump(ev_w[0], 2)

    lo, hi = linv.at[0:T, 0:128], linv.at[128:T, 128:256]
    lc = [[net.copy(v, v, dev(dx=d), track=False) for v in (lo, hi)] for d in (1, 2, -1)]

    @pl.when(x == 0)
    def _():
        linv[0:128, 128:256] = jnp.zeros((128, 128), F32)
        for cc in lc:
            for c in cc:
                c.start()

    @pl.when(x > 0)
    def _():
        linv[T:256, :] = jnp.zeros((256 - T, 256), F32)
        linv[0:128, 128:256] = jnp.zeros((128, 128), F32)

    v = rt[...].reshape(KX, 256)
    hit = iota((KX, 256), 0) + x * KX == iota((KX, 256), 1)
    v = jnp.where(iota((KX, 256), 1) < T, v * jnp.where(hit, 1.0, 0.9), 0.0)
    v = v.T
    lh[448:704, :], ll[448:704, :] = split(v)

    pump(ev_w[0], 99)
    pump(ev_w[1], 1)
    for c in xd + xf:
        c.wait_recv()
    l_at.wait()
    for i in range(4):
        v = at[i]
        same = (i == x).astype(jnp.int32)
        hit = iota((B, KX), 1) == iota((B, KX), 0) + (p * B + (1 - same) * H)
        v = v * jnp.where(hit, 1.0, 0.9)
        lh[B * i:B * (i + 1), :], ll[B * i:B * (i + 1), :] = split(v)

    for c in cu:
        c.wait_recv()

    for i, cc in enumerate(lc):
        @pl.when(x == (1, 2, 3)[i])
        def _(cc=cc):
            for c in cc:
                c.wait_recv()

    lin = split(linv[...])
    top = (p < 2).astype(F32)
    sel = jnp.where(iota((B, 256), 1) == iota((B, 256), 0) + p * B, -1.0, 0.0)
    ut = dot3(split(mxx[...].reshape(448, 256)), lin, ((1,), (1,)))
    for i in range(4):
        q[i] = ut[B * i:B * (i + 1)]
    for i in range(2):
        ug[i, y, z] = q[2 * t + i]
    topr = (r < 2).astype(F32)
    selr = jnp.where(iota((B, 256), 1) == iota((B, 256), 0) + r * B, -1.0, 0.0)
    qc = split(q[x] * (1.0 - topr) + selr * topr)
    q[0] = q[0] * (1.0 - top) + sel * top
    qg = split(q[...].reshape(448, 256))

    def product(k, j):
        n = (1 - t if j < 2 else t) * 4 + k * 2 + j % 2
        wcol = wg[:, :, :, pl.ds(pl.multiple_of(n * 256, 256), 256)].reshape(KX, 256)
        acc = dot(lh[...], wcol) + dot(ll[...], wcol)
        yv = dot3(lin, split(acc[448:704]))
        cor = dot3(qg, split(yv))
        for i in range(4):
            pc = acc[B * i:B * (i + 1)]
            if i == 0:
                pc = pc * (1.0 - top)
            pbuf[k, j, i] = (pc - cor[B * i:B * (i + 1)]) * scale

    rs = {}

    def pair_send(k, j):
        rs[k, "d", j] = net.go(pbuf.at[k, j], prx.at[k, j], dev(dt=1))

    xo, xn, xm = add(x, 2), add(x, 1), add(x, -1)

    def rs0(k):
        for j in range(2):
            rs[k, "d", j].wait_recv()
            for i in range(4):
                sb[k, i, j] = pbuf[k, 2 + j, i] + prx[k, j, i]
        rs[k, 0] = net.go(sb.at[k, xo, 0], rlr.at[k, 0], dev(dx=1))
        rs[k, 1] = net.go(sb.at[k, xo, 1], rlr.at[k, 1], dev(dx=-1))

    def rs1(k):
        rs[k, 0].wait_recv()
        sb[k, xn, 0] = sb[k, xn, 0] + rlr[k, 0]
        rs[k, 2] = net.go(sb.at[k, xn], rb.at[k, 0], dev(dx=1))
        rs[k, 1].wait_recv()
        sb[k, xm, 1] = sb[k, xm, 1] + rlr[k, 1]
        rs[k, 3] = net.go(sb.at[k, xm], rb.at[k, 1], dev(dx=-1))

    def rs2(k):
        rs[k, 2].wait_recv()
        rs[k, 3].wait_recv()
        fin[k] = sb[k, x] + (rb[k, 0] + rb[k, 1])
        rs[k, 4] = net.go(fin.at[k], finp.at[k], dev(dt=1))

    def rs3(k):
        rs[k, 4].wait_recv()
        for j in range(2):
            or_ref[:, pl.ds(pl.multiple_of(t * 1024 + k * 512 + 256 * j, 256), 256)] = fin[k, j]
            or_ref[:, pl.ds(pl.multiple_of((1 - t) * 1024 + k * 512 + 256 * j, 256), 256)] = finp[k, j]

    for j in range(4):
        product(0, j)
        if j < 2:
            pair_send(0, j)
        pump(ev_w[1], 3)
    rs0(0)
    pump(ev_w[1], 2)
    pump(ev_u, 1)
    l_ah.wait()
    xp.wait_recv()
    keep = 1.0 - topr
    hit = iota((B, HALF), 1) == iota((B, HALF), 0) + (r * B - t * HALF)
    m = ah[...] * (scale * keep) + ap[...] * (scale_p * keep)
    oh[...] = m * jnp.where(hit, 1.0, 0.9)
    rs1(0)
    pump(ev_w[1], 99)
    for j in range(4):
        product(1, j)
        if j < 2:
            pair_send(1, j)
        pump(ev_u, 3)
        if j == 2:
            rs2(0)
    rs0(1)
    pump(ev_u, 4)
    rs3(0)
    rs1(1)
    pump(ev_u, 99)
    out = []
    for i in range(2):
        for c in range(7):
            cols = slice((i * 7 + c) * 256, (i * 7 + c + 1) * 256)
            u = split(ug[i].reshape(KX, 256)[c * 256:(c + 1) * 256])
            oh[:, cols] = oh[:, cols] - dot3(qc, u, ((1,), (1,)))
        src = oh.at[:, i * KX:(i + 1) * KX]
        dst = og_ref.at[:, pl.ds(pl.multiple_of(t * HALF + i * KX, 128), KX)]
        co = pltpu.make_async_copy(src, dst, lsem.at[5 + i])
        co.start()
        out.append((co, net.go(src, dst, dev(dt=1))))
    rs2(1)
    rs3(1)
    for co, cg in out:
        co.wait()
        cg.wait_recv()
    for c in net.all:
        c.wait_send()

    @pl.when(x == 0)
    def _():
        for cc in lc:
            for c in cc:
                c.wait_send()
    assert net.n <= NCOPY, net.n


def per_device(grams, weights):
    V = pltpu.VMEM
    scratch = [
        V((4, B, KX), F32), V((2, 56, KX), F32), V((4, 4, B, DC), BF16), V((4, 4, B, 256), F32),
        V((704, KX), BF16), V((704, KX), BF16), V((4, B, 256), F32), V((4, B, 256), F32), V((2, 4, 4, B, 256), F32),
        V((2, 4, 4, B, 256), F32), V((2, 2, 4, B, 256), F32), V((2, 4, 2, B, 256), F32),
        V((2, 2, B, 256), F32), V((2, 2, 2, B, 256), F32), V((2, 2, B, 256), F32), V((2, 2, B, 256), F32),
        V((B, HALF), F32), V((B, HALF), F32), V((B, HALF), F32), V((T, 512), F32), V((256, 256), F32),
        V((2, B, 256), F32), V((2, B, 256), F32), V((B, 256), F32), V((B, 256), F32),
        V((4, 8, 128), F32), V((4, 8, 128), F32), V((4, 8, 128), F32), V((2, 8, 128), F32), V((B, 256), F32),
        pltpu.SemaphoreType.DMA((NCOPY,)), pltpu.SemaphoreType.DMA((NCOPY,)), pltpu.SemaphoreType.DMA((8,)),
    ]
    return pl.pallas_call(
        body,
        out_shape=(jax.ShapeDtypeStruct((B, H), F32), jax.ShapeDtypeStruct((B, DC), F32)),
        in_specs=[pl.BlockSpec(memory_space=pl.ANY)] * 2,
        out_specs=(pl.BlockSpec(memory_space=pl.ANY), pl.BlockSpec(memory_space=pltpu.VMEM)),
        scratch_shapes=scratch,
        compiler_params=pltpu.CompilerParams(
            collective_id=0, has_side_effects=True, vmem_limit_bytes=62 * 1024 * 1024),
    )(grams, weights)


def solution(mesh):
    torus = Mesh(mesh.devices.reshape(mesh.shape["task"], 4, 4, 4), ("task",) + ROW)
    return jax.shard_map(
        per_device, mesh=torus, in_specs=(P("task", ROW, None), P("task", ROW, None)),
        out_specs=(P(ROW, None), P(ROW, None)), check_vma=False)
```

time: 173 us -> 121 us (0.70)
  Pallas kernels: 168 us -> 114 us
    pallas_call x1, Pallas kernels: 168 us -> 114 us  [per_device(): pl.pallas_call(body, out_shape=(jax.ShapeDtypeStruct((B, H), F32), jax.Sh...]
where the time goes in v2:
time: 121 us; the launch traced here: 120 us
  Pallas kernels  114 us (94%)
  local copies, waits for them, and re-layouts  4.86 us (4%)
    pallas_call x1, Pallas kernels, per_device(): pl.pallas_call(body, out_shape=(jax.ShapeDtypeStruct((B, H), F32), jax.Sh...  114 us
    unnamed x4, local copies, waits for them, and re-layouts  4.86 us

profile of v2, /device:TPU:1, one launch (start us, length us, event | category | flops | bytes accessed | tf_op | source)
XLA Modules:
  0.0 119.6 jit_solution(9557367413220348785)
XLA Ops:
  0.6 114.1 %shard_map.41 = (f32[112,7168]{1,0:T(8,128)}, f32[112,2048]{1,0:T(8,128)}) custom-call(f32[1,112,7168]{2,1,0:T(8,128)} %a_ref.1, bf16[1,112,2048]{2,1,0:T(8,128)(2,1)} %w_ref.1), custom_call_target="tpu_custom_call" | custom-call | tf_op jit(solution)/shard_map/pallas_call | solution.py:480
  114.7 0.0 copy-start
  114.7 3.9 %copy.6 = f32[112,7168]{1,0:T(8,128)} copy(f32[112,7168]{1,0:T(8,128)} %get-tuple-element.4) | data formatting | bytes 6422528
  118.6 0.0 copy-done
  118.6 0.9 copy.7
Async XLA Ops:
  114.7 4.0 %copy-start = (f32[112,2048]{1,0:T(8,128)S(1)}, f32[112,2048]{1,0:T(8,128)}, u32[]{:S(2)}) copy-start(f32[112,2048]{1,0:T(8,128)} %get-tuple-element.5) | copy-start | bytes 2752516

commit v3 on v2

v3 whole, which is shorter than its diff:
```python
import functools

import jax
import jax.numpy as jnp
from jax import lax
from jax.experimental import pallas as pl
from jax.experimental.pallas import tpu as pltpu
from jax.sharding import Mesh
from jax.sharding import PartitionSpec as P

ROW = ("row_0", "row_1", "row_2")
F32 = jnp.float32
BF16 = jnp.bfloat16
B = 112
T = 224
H = 7168
DC = 2048
KX = 1792
HALF = 3584
MESH = pl.DeviceIdType.MESH
HI = lax.Precision.HIGHEST
NCOPY = 216
NSEND = 200
CHUNKS = (512, 512)
NK = len(CHUNKS)


class Net:
    def __init__(self, send, recv):
        self.send, self.recv, self.n, self.all, self.sends, self.free = send, recv, 0, [], 0, []

    def copy(self, src, dst, dev, track=True, like=None):
        i = self.n
        self.n += 1
        k = i if like is None else like
        if self.free:
            j = self.free.pop()
        else:
            j = self.sends
            self.sends += 1
        c = pltpu.make_async_remote_copy(
            src_ref=src, dst_ref=dst, send_sem=self.send.at[j], recv_sem=self.recv.at[k],
            device_id=dev, device_id_type=MESH)
        if track:
            self.all.append((c, j))
        return c

    def retire(self, n):
        for c, j in self.all[:n]:
            c.wait_send()
            self.free.append(j)
        del self.all[:n]

    def go(self, src, dst, dev):
        c = self.copy(src, dst, dev)
        c.start()
        return c


def iota(shape, dim):
    return lax.broadcasted_iota(jnp.int32, shape, dim)


def dot(a, b, dims=((1,), (0,)), precision=None):
    return lax.dot_general(a, b, (dims, ((), ())), precision=precision, preferred_element_type=F32)


def split(v):
    hi = v.astype(BF16)
    return hi, (v - hi.astype(F32)).astype(BF16)


def dot3(a, b, dims=((1,), (0,))):
    return dot(a[0], b[0], dims) + (dot(a[0], b[1], dims) + dot(a[1], b[0], dims))


GROUPS = dict(opp=(0, B, 592), z=(224, 256, 0), p1=(736, B, 368), m1=(960, B, 480), own=(1184, B, 256))


def chol_steps(g, linv, corner):
    nb = 32

    def start():
        linv[T:256, 0:128] = jnp.zeros((256 - T, 128), F32)
        linv[T:256, 128:256] = jnp.zeros((256 - T, 128), F32)
        for i in range(2):
            g[B * i:B * (i + 1), 0:256] = corner(i)
        g[:, 256:512] = jnp.where(iota((T, 256), 0) == iota((T, 256), 1), 1.0, 0.0)

    def step(b):
        rid = iota((nb, 128), 0)
        k0 = nb * b
        left = [i for i in (0, 1) if 128 * (i + 1) > k0]
        tiles = left + [2] + ([3] if k0 + nb > 128 else [])
        v = {i: g[k0:k0 + nb, 128 * i:128 * i + 128] for i in tiles}

        def column(k):
            i = k // 128
            return jnp.broadcast_to(v[i][:, k % 128:k % 128 + 1], (nb, 128))

        for j in range(0, nb, 2):
            c0, c1 = column(k0 + j), column(k0 + j + 1)
            d00, d01, d11 = c0[j:j + 1], c1[j:j + 1], c1[j + 1:j + 2]
            inv = 1.0 / (d00 * d11 - d01 * d01)
            f0 = jnp.where(rid > j + 1, (d11 * inv) * c0 - (d01 * inv) * c1, 0.0)
            f1 = jnp.where(rid > j + 1, (d00 * inv) * c1 - (d01 * inv) * c0, 0.0)
            f0 = jnp.where(rid == j + 1, d01 / d00, f0)
            for i in tiles:
                v[i] = v[i] - f0 * v[i][j:j + 1, :] - f1 * v[i][j + 1:j + 2, :]
        dg = 0.0
        for i in left:
            dg = dg + jnp.sum(jnp.where(iota((nb, 128), 1) + 128 * i == rid + k0, v[i], 0.0), axis=1, keepdims=True)
        sc = 1.0 / jnp.sqrt(dg)
        for i in tiles:
            v[i] = v[i] * sc
        linv[k0:k0 + nb, 0:128] = v[2]
        if 3 in v:
            linv[k0:k0 + nb, 128:256] = v[3]
        if k0 + nb < T:
            lo = 128 if k0 + nb >= 128 else 0
            lhs = jnp.concatenate([v[i] for i in left if 128 * i >= lo], axis=1)
            off = k0 + nb - lo
            for i in tiles:
                if 128 * (i + 1) > lo:
                    cols = slice(128 * i, 128 * i + 128)
                    upd = dot(lhs, v[i], ((0,), (0,)), HI)
                    g[k0 + nb:T, cols] = g[k0 + nb:T, cols] - upd[off:off + T - k0 - nb, :]

    return [start] + [functools.partial(step, b) for b in range(T // nb)]


def body(a_ref, w_ref, og_ref, or_ref,
         at, bnc, wg, rt, lhs, mxx, q, ug, *rest):
    pbuf, prx, sb, rlr, rb, fin, finp = (rest[NK * i:NK * (i + 1)] for i in range(7))
    (ah, ap, oh, pacc, g, linv, sx, sr, mx, mr, trx, try_, trz, trp, dw, send, recv, lsem) = rest[7 * NK:]
    t = lax.axis_index("task")
    x, y, z = (lax.axis_index(n) for n in ROW)
    p = y * 4 + z
    r = x * 16 + p

    def add(v, d):
        return lax.rem(v + (4 + d), 4)

    def dev(dt=0, dx=0, dy=0, dz=0):
        return (1 - t if dt else t, add(x, dx) if dx else x, add(y, dy) if dy else y, add(z, dz) if dz else z)

    net = Net(send, recv)
    ws = pl.multiple_of((r * 7 // 8 - r // 63) * 128, 128)
    kx = pl.multiple_of(x * KX, 128)
    hc = pl.multiple_of(t * HALF, 128)
    hp = pl.multiple_of((1 - t) * HALF, 128)
    loads = [(a_ref.at[0, :, pl.ds(ws, 256)], dw), (a_ref.at[0, :, 0:256], rt.at[y, z]), (w_ref.at[0], wg.at[y, z]),
             (a_ref.at[0, :, pl.ds(kx, KX)], at.at[x]), (a_ref.at[0, :, pl.ds(hc, HALF)], ah)]
    loads = [pltpu.make_async_copy(a, b, lsem.at[i]) for i, (a, b) in enumerate(loads)]
    l_dw, l_rt, l_w, l_at, l_ah = loads
    for c in loads:
        c.start()
    bar = pltpu.get_barrier_semaphore()
    peers = [dev(dt=1)] + [dev(**{a: d}) for a in ("dx", "dy", "dz") for d in (1, -1, 2)]
    for d in peers:
        pl.semaphore_signal(bar, inc=1, device_id=d, device_id_type=MESH)
    pl.semaphore_wait(bar, len(peers))

    def spread(buf, val, pos, axis):
        buf[pos] = jnp.broadcast_to(val, (8, 128))
        return [net.go(buf.at[pos], buf.at[pos], dev(**{axis: d})) for d in (1, -1, 2)]

    def total(buf, copies):
        for c in copies:
            c.wait_recv()
        return buf[0] + buf[1] + (buf[2] + buf[3])

    def gather(sl):
        def nb(h, stage, d):
            axis = ("dy", "dz")[(h + stage) % 2]
            return dev(**{axis: d})

        def ref(h, part, a, b):
            return sl(h, part, a, b) if h == 0 else sl(h, part, b, a)

        first, second = (y, z), (z, y)
        st = {}

        def ph1(h):
            s = ref(h, None, first[h], second[h])
            st[h, "p"] = net.go(s, s, nb(h, 0, 1))
            st[h, "m"] = net.go(s, s, nb(h, 0, -1))

        def ph2(h, k, a):
            s = ref(h, None, a, second[h])
            st[h, k, "p"] = net.go(s, s, nb(h, 1, 1))
            st[h, k, "m"] = net.go(s, s, nb(h, 1, -1))

        def fw1(h, side):
            d = -1 if side == "p" else 1
            st[h, side].wait_recv()
            s = ref(h, 0 if side == "p" else 1, add(first[h], d), second[h])
            st[h, "f" + side] = net.go(s, s, nb(h, 0, -d))

        def end1(h):
            st[h, "fp"].wait_recv()
            st[h, "fm"].wait_recv()

        def fw2(h, k, a, side):
            d = -1 if side == "p" else 1
            st[h, k, side].wait_recv()
            s = ref(h, 0 if side == "p" else 1, a, add(second[h], d))
            st[h, k, "f" + side] = net.go(s, s, nb(h, 1, -d))

        def end2(h, k):
            st[h, k, "fp"].wait_recv()
            st[h, k, "fm"].wait_recv()

        both = (0, 1)
        idx = {k: (lambda h, d=d: add(first[h], d) if d else first[h]) for k, d in ((0, 0), (1, -1), (2, 1), (3, 2))}

        def far(k):
            return [lambda h=h, side=side: fw2(h, k, idx[k](h), side) for h in both for side in "pm"]

        return dict(
            start=[lambda: [ph1(h) for h in both]],
            own=[lambda: [ph2(h, 0, first[h]) for h in both]],
            fw1=[lambda h=h, side=side: fw1(h, side) for side in "pm" for h in both],
            near=[lambda h=h, k=k: ph2(h, k, idx[k](h)) for k in (1, 2) for h in both],
            opp=[lambda h=h: (end1(h), ph2(h, 3, idx[3](h))) for h in both],
            f0=far(0), f1=far(1), f2=far(2), f3=far(3),
            end=[lambda: [end2(h, k) for k in range(4) for h in both]])

    def sl_rt(h, part, a, b):
        rows = slice(None) if part is None else pl.ds(56 * part, 56)
        return rt.at[a, b, rows, pl.ds(128 * h, 128)]

    def sl_w(k, h, part, a, b):
        lo, n = 1024 * h + sum(CHUNKS[:k]), CHUNKS[k]
        if part is not None:
            lo, n = lo + n // 2 * part, n // 2
        return wg.at[a, b, :, pl.ds(lo, n)]

    def sl_u(h, part, a, b):
        blk = slice(None) if part is None else part
        return ug.at[blk, a, b, :, pl.ds(128 * h, 128)]

    ev_r = gather(sl_rt)
    ev_w = [gather(functools.partial(sl_w, k)) for k in range(NK)]
    ev_u = gather(sl_u)

    def order(e, *names):
        return [f for n in names for f in e[n]]

    ev_r = order(ev_r, "start", "own", "fw1", "near", "f0", "opp", "f1", "f2", "f3", "end")

    def pump(ev, n=1):
        for _ in range(min(n, len(ev))):
            ev.pop(0)()

    l_dw.wait()
    tile = iota((B, 256), 1) == iota((B, 256), 0) + (r * B - ws)
    part = jnp.sum(jnp.where(tile, dw[...], 0.0), axis=1, keepdims=True)
    part = jnp.sum(part, axis=0, keepdims=True)
    cs = spread(trx, part, x, "dx")
    l_rt.wait()
    pump(ev_r, 2)

    def acol(d):
        return pl.ds(pl.multiple_of(add(x, d) * KX, 128), KX)

    n_early = len(net.all)
    xb = [net.go(a_ref.at[0, 0:56, acol(2)], bnc.at[0], dev(dx=1)),
          net.go(a_ref.at[0, 56:112, acol(2)], bnc.at[1], dev(dx=-1))]
    xd = [net.go(a_ref.at[0, :, acol(1)], at.at[x], dev(dx=1)),
          net.go(a_ref.at[0, :, acol(-1)], at.at[x], dev(dx=-1))]
    xp = net.go(a_ref.at[0, :, pl.ds(hp, HALF)], ap, dev(dt=1))
    xf = []
    l_w.wait()
    ev_w[0]["start"][0]()

    def relay0():
        xb[0].wait_recv()
        xf.append(net.go(bnc.at[0], at.at[add(x, -1), 0:56], dev(dx=1)))

    def relay1():
        xb[1].wait_recv()
        xf.append(net.go(bnc.at[1], at.at[add(x, 1), 56:112], dev(dx=-1)))

    ev_a = [relay0, relay1]

    old = []
    s = total(trx, cs)
    cs = spread(try_, s, y, "dy")
    a0 = len(net.all)
    pump(ev_r, 8)
    old += [c for c, _ in net.all[a0:]]
    ev_w[0]["own"][0]()
    s = total(try_, cs)
    cs = spread(trz, s, z, "dz")
    a0 = len(net.all)
    pump(ev_r, 6)
    old += [c for c, _ in net.all[a0:]]
    s = total(trz, cs)
    scale8 = float(H) / s
    trp[0] = scale8
    cp = net.go(trp.at[0], trp.at[1], dev(dt=1))
    scale = scale8[0:1, 0:1]
    for e in [ev_w[0]["fw1"], ev_w[0]["near"][:2], []]:
        for f in e:
            f()
        a0 = len(net.all)
        pump(ev_r, 4)
        old += [c for c, _ in net.all[a0:]]
    a0 = len(net.all)
    pump(ev_r, 99)
    old += [c for c, _ in net.all[a0:]]

    lane = iota((B, 256), 1)
    hit = lane == iota((B, 256), 0) + r * B
    mx[...] = jnp.where(lane < T, rt[y, z] * jnp.where(hit, scale, 0.9 * scale), 0.0)
    cm = net.go(mx, mr, dev(dt=1))
    for i in range(2):
        hit = lane == iota((B, 256), 0) + i * B
        sx[i] = jnp.where(lane < T, rt[0, i] * jnp.where(hit, scale, 0.9 * scale), 0.0)
    cS = net.go(sx, sr, dev(dt=1))
    cp.wait_recv()
    scale_p = trp[1][0:1, 0:1]
    cm.wait_recv()
    mxx[x] = mx[...] + mr[...]
    mine = pl.ds(pl.multiple_of(t * 56, 8), 56)
    cu = [net.go(mxx.at[x, mine], mxx.at[x, mine], dev(dx=d)) for d in (1, -1, 2)]
    pump(ev_a, 2)
    cS.wait_recv()

    net.retire(n_early)
    late = [c for c in net.all if any(c[0] is d for d in old)]
    net.all = late + [c for c in net.all if not any(c[0] is d for d in old)]
    net.retire(len(late))
    w0, w1 = ev_w
    ev = (w0["near"][2:] + w1["start"] + order(w0, "f0", "opp", "f1") + w1["own"] + w0["f2"] + w1["fw1"]
          + order(w0, "f3", "end") + order(w1, "opp", "near", "f0"))

    def until(e):
        while any(v is e["end"][0] for v in ev):
            pump(ev)

    for f in chol_steps(g, linv, lambda i: sx[i] + sr[i]):
        pl.when(x == 0)(f)
        pump(ev, 3)

    regions = [linv.at[pl.ds(pl.multiple_of(B * t, 8), B), 0:128],
               linv.at[pl.ds(pl.multiple_of(128 + 48 * t, 8), 48), 128:256]]
    lc, lp = [], []
    for v in regions:
        first = net.n
        lc.append([net.copy(v, v, dev(dx=d), track=False, like=first) for d in (1, 2, -1)])
    for v in regions:
        lp.append(net.copy(v, v, dev(dt=1), track=False))

    @pl.when(x == 0)
    def _():
        linv[0:128, 128:256] = jnp.zeros((128, 128), F32)
        for cc in lc:
            for c in cc:
                c.start()

    @pl.when(x > 0)
    def _():
        linv[T:256, :] = jnp.zeros((256 - T, 256), F32)
        linv[0:128, 128:256] = jnp.zeros((128, 128), F32)

    v = rt[...].reshape(KX, 256)
    hit = iota((KX, 256), 0) + x * KX == iota((KX, 256), 1)
    v = jnp.where(iota((KX, 256), 1) < T, v * jnp.where(hit, 1.0, 0.9), 0.0)
    v = v.T

    def put(name, v):
        o, m, _ = GROUPS[name]
        lhs[o:o + m, :], lhs[o + m:o + 2 * m, :] = split(v)

    put("z", v)
    pump(ev, 3)

    def tile_in(name, d):
        v = at[add(x, d)]
        if d == 0:
            hit = iota((B, KX), 1) == iota((B, KX), 0) + p * B
            v = v * jnp.where(hit, 1.0, 0.9)
        else:
            v = v * 0.9
        put(name, v)

    l_at.wait()
    tile_in("own", 0)
    xd[1].wait_recv()
    tile_in("p1", 1)
    xd[0].wait_recv()
    tile_in("m1", -1)

    def rows_of(k, j, *names):
        n = CHUNKS[k]
        lo = pl.multiple_of((t if j else 1 - t) * 1024 + sum(CHUNKS[:k]), 256)
        wcol = wg[:, :, :, pl.ds(lo, n)].reshape(KX, n)
        first = GROUPS[names[0]][0]
        last, m, _ = GROUPS[names[-1]]
        acc = dot(lhs[first:last + 2 * m], wcol)
        for name in names:
            o, m, to = GROUPS[name]
            o = o - first
            pacc[j, to:to + m, 0:n] = acc[o:o + m] + acc[o + m:o + 2 * m]

    until(w0)
    early = [(j, names) for j in range(2) for names in (("z",), ("p1", "m1", "own"))]
    rows_of(0, 0, *early[0][1])
    pump(ev, 2)
    for c in cu:
        c.wait_recv()
    cv = []
    for d in (1, -1, 2):
        v = mxx.at[add(x, d), mine]
        cv.append(net.go(v, v, dev(dt=1)))

    @pl.when(x > 0)
    def _():
        for cc in lc:
            cc[0].wait_recv()
        for c in lp:
            c.start()
        for c in lp:
            c.wait_recv()

    pump(ev, 2)
    for c in cv:
        c.wait_recv()

    lin = split(linv[...])
    ut = dot3(split(mxx[...].reshape(448, 256)), lin, ((1,), (1,)))
    for i in range(4):
        q[i] = ut[B * i:B * (i + 1)]
    for i in range(2):
        ug[i, y, z] = q[2 * t + i]
    ev += (order(w1, "f3", "f1", "f2") + order(ev_u, "start", "own") + w1["end"]
           + order(ev_u, "fw1", "near", "opp", "f0", "f1", "f2", "f3", "end"))
    ident = iota((B, 256), 1) - iota((B, 256), 0)

    def rows_q(d):
        xx = add(x, d)
        top = (xx * 16 + p < 2).astype(F32)
        sel = jnp.where(ident == p * B, -1.0, 0.0)
        return q[xx] * (1.0 - top) + sel * top, 1.0 - top

    qs = [rows_q(d) for d in (0, 1, -1, 2)]
    keep = qs[0][1]
    qc = split(qs[0][0])
    qg = split(jnp.concatenate([v for v, _ in qs], axis=0))

    ys = {}

    def solve(k, j):
        ys[k, j] = split(dot3(lin, split(pacc[j, 0:256, 0:CHUNKS[k]])))

    def correct(k, j, lo, hi):
        n = CHUNKS[k]
        cor = dot3([v[B * lo:B * hi] for v in qg], ys[k, j])
        for i in range(lo, hi):
            pc = pacc[j, 256 + B * i:256 + B * (i + 1), 0:n] * qs[i][1]
            pbuf[k][j, i] = (pc - cor[B * (i - lo):B * (i + 1 - lo)]) * scale

    rs = {}

    def pair_send(k, lo, hi):
        rs[k, "d", lo] = net.go(pbuf[k].at[0, lo:hi], prx[k].at[lo:hi], dev(dt=1))

    def pair_sum(k, lo, hi):
        rs[k, "d", lo].wait_recv()
        n = CHUNKS[k] // 2
        for i in range(lo, hi):
            for j in range(2):
                cols = slice(n * j, n * j + n)
                sb[k][i, j] = pbuf[k][1, i, :, cols] + prx[k][i, :, cols]

    def rs0(k):
        rs[k, 0] = net.go(sb[k].at[3, 0], rlr[k].at[0], dev(dx=1))
        rs[k, 1] = net.go(sb[k].at[3, 1], rlr[k].at[1], dev(dx=-1))

    def rs1(k):
        rs[k, 0].wait_recv()
        sb[k][1, 0] = sb[k][1, 0] + rlr[k][0]
        rs[k, 2] = net.go(sb[k].at[1], rb[k].at[0], dev(dx=1))
        rs[k, 1].wait_recv()
        sb[k][2, 1] = sb[k][2, 1] + rlr[k][1]
        rs[k, 3] = net.go(sb[k].at[2], rb[k].at[1], dev(dx=-1))

    def rs2(k):
        rs[k, 2].wait_recv()
        rs[k, 3].wait_recv()
        fin[k][...] = sb[k][0] + (rb[k][0] + rb[k][1])
        rs[k, 4] = net.go(fin[k], finp[k], dev(dt=1))

    def rs3(k):
        rs[k, 4].wait_recv()
        n = CHUNKS[k] // 2
        for j in range(2):
            lo = sum(CHUNKS[:k]) + n * j
            or_ref[:, pl.ds(pl.multiple_of(t * 1024 + lo, 128), n)] = fin[k][j]
            or_ref[:, pl.ds(pl.multiple_of((1 - t) * 1024 + lo, 128), n)] = finp[k][j]

    for j, names in early[1:]:
        rows_of(0, j, *names)
        pump(ev, 2)
    for c in xf:
        c.wait_recv()
    tile_in("opp", 2)
    for j in range(2):
        rows_of(0, j, "opp")
    for j in range(2):
        solve(0, j)
        correct(0, j, 0, 4)
        if j == 0:
            pair_send(0, 0, 4)
        pump(ev, 2)
    pair_sum(0, 0, 4)
    rs0(0)
    l_ah.wait()
    xp.wait_recv()
    hit = iota((B, HALF), 1) == iota((B, HALF), 0) + (r * B - t * HALF)
    m = ah[...] * (scale * keep) + ap[...] * (scale_p * keep)
    oh[...] = m * jnp.where(hit, 1.0, 0.9)
    pump(ev, 4)
    until(w1)
    for j in range(2):
        rows_of(1, j, "opp", "z")
        solve(1, j)
        correct(1, j, 3, 4)
        if j == 0:
            pair_send(1, 3, 4)
            rs1(0)
        pump(ev, 3)
    pair_sum(1, 3, 4)
    rs0(1)
    for j in range(2):
        rows_of(1, j, "p1", "m1")
        correct(1, j, 1, 3)
        if j == 0:
            pair_send(1, 1, 3)
        pump(ev, 4)
    pair_sum(1, 1, 3)
    rs1(1)
    for j in range(2):
        rows_of(1, j, "own")
        correct(1, j, 0, 1)
        if j == 0:
            pair_send(1, 0, 1)
        pump(ev, 5)
    pair_sum(1, 0, 1)
    rs2(0)
    pump(ev, 3)
    rs3(0)
    pump(ev, 99)
    out = []
    for i in range(2):
        for c in range(7):
            cols = slice((i * 7 + c) * 256, (i * 7 + c + 1) * 256)
            u = split(ug[i].reshape(KX, 256)[c * 256:(c + 1) * 256])
            oh[:, cols] = oh[:, cols] - dot3(qc, u, ((1,), (1,)))
        src = oh.at[:, i * KX:(i + 1) * KX]
        dst = og_ref.at[:, pl.ds(pl.multiple_of(t * HALF + i * KX, 128), KX)]
        co = pltpu.make_async_copy(src, dst, lsem.at[5 + i])
        co.start()
        out.append((co, net.go(src, dst, dev(dt=1))))
        if i == 0:
            rs2(1)
    rs3(1)
    for co, cg in out:
        co.wait()
        cg.wait_recv()
    net.retire(len(net.all))

    @pl.when(x == 0)
    def _():
        for cc in lc:
            for c in cc:
                c.wait_send()

    @pl.when(x > 0)
    def _():
        for c in lp:
            c.wait_send()

    assert net.n <= NCOPY and net.sends <= NSEND, (net.n, net.sends)


def per_device(grams, weights):
    V = pltpu.VMEM
    scratch = [
        V((4, B, KX), F32), V((2, 56, KX), F32), V((4, 4, B, DC), BF16), V((4, 4, B, 256), F32),
        V((1408, KX), BF16), V((4, B, 256), F32), V((4, B, 256), F32), V((2, 4, 4, B, 256), F32),
        *[V((2, 4, B, n), F32) for n in CHUNKS], *[V((4, B, n), F32) for n in CHUNKS],
        *[V((4, 2, B, n // 2), F32) for n in CHUNKS], *[V((2, B, n // 2), F32) for n in CHUNKS],
        *[V((2, 2, B, n // 2), F32) for n in CHUNKS], *[V((2, B, n // 2), F32) for n in CHUNKS],
        *[V((2, B, n // 2), F32) for n in CHUNKS],
        V((B, HALF), F32), V((B, HALF), F32), V((B, HALF), F32), V((2, 704, 512), F32), V((T, 512), F32), V((256, 256), F32),
        V((2, B, 256), F32), V((2, B, 256), F32), V((B, 256), F32), V((B, 256), F32),
        V((4, 8, 128), F32), V((4, 8, 128), F32), V((4, 8, 128), F32), V((2, 8, 128), F32), V((B, 256), F32),
        pltpu.SemaphoreType.DMA((NSEND,)), pltpu.SemaphoreType.DMA((NCOPY,)), pltpu.SemaphoreType.DMA((8,)),
    ]
    return pl.pallas_call(
        body,
        out_shape=(pltpu.VMEM((B, H), F32), pltpu.VMEM((B, DC), F32)),
        in_specs=[pl.BlockSpec(memory_space=pl.ANY)] * 2,
        out_specs=(pl.BlockSpec(memory_space=pltpu.VMEM), pl.BlockSpec(memory_space=pltpu.VMEM)),
        scratch_shapes=scratch,
        compiler_params=pltpu.CompilerParams(
            collective_id=0, has_side_effects=True, vmem_limit_bytes=57 * 1024 * 1024),
    )(grams, weights)


def solution(mesh):
    torus = Mesh(mesh.devices.reshape(mesh.shape["task"], 4, 4, 4), ("task",) + ROW)
    return jax.shard_map(
        per_device, mesh=torus, in_specs=(P("task", ROW, None), P("task", ROW, None)),
        out_specs=(P(ROW, None), P(ROW, None)), check_vma=False)
```

time: 121 us -> 97 us (0.80); the launches traced: 120 us -> 96.8 us
  Pallas kernels: 114 us -> 93.6 us
  local copies, waits for them, and re-layouts: 4.86 us -> 2.61 us
    pallas_call x1, Pallas kernels: 114 us -> 93.6 us  [per_device(): pl.pallas_call(body, out_shape=(pltpu.VMEM((B, H), F32), pltpu.VMEM((B, D...]
    unnamed x4 -> x2, local copies, waits for them, and re-layouts: 4.86 us -> 2.61 us
where the time goes in v3:
time: 97 us; the launch traced here: 96.8 us
  Pallas kernels  93.6 us (96%)
  local copies, waits for them, and re-layouts  2.61 us (3%)
    pallas_call x1, Pallas kernels, per_device(): pl.pallas_call(body, out_shape=(pltpu.VMEM((B, H), F32), pltpu.VMEM((B, D...  93.6 us
    unnamed x2, local copies, waits for them, and re-layouts  2.61 us

profile of v3, /device:TPU:1, one launch (start us, length us, event | category | flops | bytes accessed | tf_op | source)
XLA Modules:
  0.0 96.8 jit_solution(10501479937259447641)
XLA Ops:
  0.6 93.6 %shard_map.41 = (f32[112,7168]{1,0:T(8,128)S(1)}, f32[112,2048]{1,0:T(8,128)S(1)}) custom-call(f32[1,112,7168]{2,1,0:T(8,128)} %a_ref.1, bf16[1,112,2048]{2,1,0:T(8,128)(2,1)} %w_ref.1), custom_call_target="tpu_custom_call" | custom-call | tf_op jit(solution)/shard_map/pallas_call | solution.py:603
  94.2 1.7 %copy.6 = f32[112,7168]{1,0:T(8,128)} copy(f32[112,7168]{1,0:T(8,128)S(1)} %get-tuple-element.2) | data formatting | bytes 6422528
  95.9 0.9 copy.7

commit v4 on v3

--- a/solution.py
+++ b/solution.py
@@ -408,7 +408,7 @@
     until(w0)
     early = [(j, names) for j in range(2) for names in (("z",), ("p1", "m1", "own"))]
     rows_of(0, 0, *early[0][1])
-    pump(ev, 2)
+    pump(ev, 6)
     for c in cu:
         c.wait_recv()
     cv = []
@@ -554,11 +554,13 @@
     rs3(0)
     pump(ev, 99)
     out = []
+    q2 = jnp.concatenate(qc, axis=0)
     for i in range(2):
         for c in range(7):
             cols = slice((i * 7 + c) * 256, (i * 7 + c + 1) * 256)
             u = split(ug[i].reshape(KX, 256)[c * 256:(c + 1) * 256])
-            oh[:, cols] = oh[:, cols] - dot3(qc, u, ((1,), (1,)))
+            d = dot(q2, u[0], ((1,), (1,)))
+            oh[:, cols] = oh[:, cols] - (d[0:B] + d[B:2 * B]) - dot(qc[0], u[1], ((1,), (1,)))
         src = oh.at[:, i * KX:(i + 1) * KX]
         dst = og_ref.at[:, pl.ds(pl.multiple_of(t * HALF + i * KX, 128), KX)]
         co = pltpu.make_async_copy(src, dst, lsem.at[5 + i])

time: 97 us -> 96.1 us (level)
  no operation moved by 1% of the time
where the time goes in v4:
time: 96.1 us; the launch traced here: 96 us
  Pallas kernels  92.7 us (96%)
  local copies, waits for them, and re-layouts  2.61 us (3%)
    pallas_call x1, Pallas kernels, per_device(): pl.pallas_call(body, out_shape=(pltpu.VMEM((B, H), F32), pltpu.VMEM((B, D...  92.7 us
    unnamed x2, local copies, waits for them, and re-layouts  2.61 us

profile of v4, /device:TPU:1, one launch (start us, length us, event | category | flops | bytes accessed | tf_op | source)
XLA Modules:
  0.0 96.0 jit_solution(12862113767007235912)
XLA Ops:
  0.6 92.7 %shard_map.41 = (f32[112,7168]{1,0:T(8,128)S(1)}, f32[112,2048]{1,0:T(8,128)S(1)}) custom-call(f32[1,112,7168]{2,1,0:T(8,128)} %a_ref.1, bf16[1,112,2048]{2,1,0:T(8,128)(2,1)} %w_ref.1), custom_call_target="tpu_custom_call" | custom-call | tf_op jit(solution)/shard_map/pallas_call | solution.py:605
  93.3 1.7 %copy.6 = f32[112,7168]{1,0:T(8,128)} copy(f32[112,7168]{1,0:T(8,128)S(1)} %get-tuple-element.2) | data formatting | bytes 6422528
  95.0 0.9 copy.7
